TPU v7x, 128 devices: a whole 4x4x4 slice. The times are simulated.
128 devices in a mesh: dp: 8 (over x, core), seq: 16 (over z, y).
Axes of the slice: x: 4, y: 4, z: 4, core: 2. Of those that a mesh axis runs over, the one named last changes fastest.
Arguments:
- text_rows: bfloat16 [16384, 8192], P(('dp', 'seq')), may hold values from -6 to 6
- image_rows: bfloat16 [32, 256, 8192], P('dp', 'seq'), may hold values from -6 to 6
- tile_group: int32 [32], replicated, may hold values from 0 to 7, as said below
- tile_offset: int32 [32], replicated, may hold values from 0 to 1792, as said below
- seq_len: int32 [8], P('dp'), may hold values from 1024 to 2048, as said below
- doc_ids: int32 [8, 2048], P('dp'), may hold values from 0 to 7, never falling along the last dimension, each value on 1 to 512 neighbouring positions
- norm_gain: float32 [8192], replicated, may hold values from 0.1 to 1.9
- q_weight: bfloat16 [8192, 8192], P(None, 'seq'), may hold values from -0.0625 to 0.0625
- k_weight: bfloat16 [8192, 1024], P(None, 'seq'), may hold values from -0.0625 to 0.0625
- v_weight: bfloat16 [8192, 1024], P(None, 'seq'), may hold values from -0.0625 to 0.0625
- q_bias: float32 [8192], P('seq'), may hold values from -3 to 3
- k_bias: float32 [1024], P('seq'), may hold values from -40 to 40
- v_bias: float32 [1024], P('seq'), may hold values from -3 to 3
Outputs:
- attention: bfloat16 [16384, 8192], P('dp', 'seq')
Inputs may be any that keep to these rules, and one draw needn't show every extreme that they name: `tile_group`: the 4 tiles r * 4 to r * 4 + 3 of each r < 8 go to distinct packed sequences; one packed sequence takes exactly 7 tiles and none takes more. `tile_offset`: the tiles of one packed sequence lie back to back in increasing tile order and end at or before its seq_len. `seq_len`: some packed sequence uses all 2048 positions. `doc_ids`: document ids never fall along a sequence and no document is longer than 512 positions.
All inputs are finite; a program needn't handle non-finite values.
Results may differ from a plain program's by a relative error of at most 0.003.
The roundings to bfloat16 on the way count: a program that leaves them out, or rounds other values in their place, can miss the bound.
Values may be sent and summed in bfloat16 or wider, within the bound.
No kernel may reach another device: no remote copies, remote signals or barrier semaphores. Data moves between devices by JAX's collectives and lax.ppermute only.
A program may use at most 128 MiB of HBM per device.

v0:
```python
import jax
import jax.numpy as jnp
from jax import lax
from jax.sharding import PartitionSpec as P

TR = 256
THETA = 1000000.0
NEGATIVE = -1e30
EPSILON = 1e-06


def swapped(block, axis, bit):
    count = lax.axis_size(axis)
    route = []
    for low in range(count):
        high = low | 1 << bit
        if high != low and high < count:
            route += [(low, high), (high, low)]
    return lax.ppermute(block, axis, route)


def rms_norm(row_block, norm_gain):
    float_rows = row_block.astype(jnp.float32)
    inv_rms = lax.rsqrt(jnp.mean(float_rows * float_rows, axis=-1, keepdims=True) + EPSILON)
    return (float_rows * inv_rms * norm_gain).astype(jnp.bfloat16)


def doc_positions(doc_row):
    indices = jnp.arange(doc_row.shape[0], dtype=jnp.int32)
    starts = jnp.concatenate([jnp.ones((1,), jnp.bool_), doc_row[1:] != doc_row[:-1]])
    first_index = lax.cummax(jnp.where(starts, indices, 0), axis=0)
    return indices - first_index


def rotary(values, position):
    head_dim = values.shape[-1]
    half_dim = head_dim // 2
    frequency = THETA ** (-(jnp.arange(half_dim, dtype=jnp.float32) * 2.0) / head_dim)
    angles = position.astype(jnp.float32)[:, None] * frequency[None, :]
    cosine = jnp.concatenate([jnp.cos(angles), jnp.cos(angles)], axis=-1)
    sine_part = jnp.concatenate([jnp.sin(angles), jnp.sin(angles)], axis=-1)
    if values.ndim == 3:
        cosine = cosine[:, None, :]
        sine_part = sine_part[:, None, :]
    rotated = jnp.concatenate([-values[..., half_dim:], values[..., :half_dim]], axis=-1)
    return values * cosine + rotated * sine_part


def attend(queries, key_rows, value_rows, doc_row, valid_len):
    length, head_count, head_dim = queries.shape
    window = length // 4
    block_rows = min(512, length)
    scale_factor = head_dim ** (-0.5)
    keys_pad = jnp.concatenate([jnp.zeros((window, head_dim), key_rows.dtype), key_rows], axis=0)
    values_pad = jnp.concatenate(
        [jnp.zeros((window, head_dim), value_rows.dtype), value_rows], axis=0
    )
    doc_pad = jnp.concatenate([jnp.full((window,), -1, jnp.int32), doc_row])
    index_pad = jnp.arange(length + window, dtype=jnp.int32) - window

    def one_block(block_step, output):
        row_start = block_step * block_rows
        query_part = lax.dynamic_slice_in_dim(queries, row_start, block_rows, 0)
        key_part = lax.dynamic_slice_in_dim(keys_pad, row_start, block_rows + window, 0)
        value_part = lax.dynamic_slice_in_dim(values_pad, row_start, block_rows + window, 0)
        doc_part = lax.dynamic_slice_in_dim(doc_pad, row_start, block_rows + window, 0)
        key_index = lax.dynamic_slice_in_dim(index_pad, row_start, block_rows + window, 0)
        query_doc = lax.dynamic_slice_in_dim(doc_row, row_start, block_rows, 0)
        query_index = row_start + jnp.arange(block_rows, dtype=jnp.int32)
        scores = (
            jnp.einsum("qhd,kd->hqk", query_part, key_part, preferred_element_type=jnp.float32)
            * scale_factor
        )
        allowed = (
            (query_doc[:, None] == doc_part[None, :])
            & (key_index[None, :] <= query_index[:, None])
            & (key_index[None, :] < valid_len)
        )
        scores = jnp.where(allowed[None], scores, NEGATIVE)
        row_peak = jnp.max(scores, axis=-1, keepdims=True)
        exponent = jnp.exp(scores - row_peak)
        weights = (exponent / jnp.sum(exponent, axis=-1, keepdims=True)).astype(jnp.bfloat16)
        mixed = jnp.einsum("hqk,kd->qhd", weights, value_part, preferred_element_type=jnp.float32)
        mixed = jnp.where((query_index < valid_len)[:, None, None], mixed, 0.0).astype(jnp.bfloat16)
        return lax.dynamic_update_slice_in_dim(
            output, mixed.reshape(block_rows, head_count * head_dim), row_start, 0
        )

    initial = jnp.zeros((length, head_count * head_dim), jnp.bfloat16)
    return lax.fori_loop(0, length // block_rows, one_block, initial)


def per_device(
    text_rows,
    image_rows,
    tile_group,
    tile_offset,
    seq_len,
    doc_ids,
    norm_gain,
    q_weight,
    k_weight,
    v_weight,
    q_bias,
    k_bias,
    v_bias,
):
    group_count = lax.axis_size("dp")
    member_count = lax.axis_size("seq")
    my_group = lax.axis_index("dp")
    my_member = lax.axis_index("seq")
    tiles_row, piece_rows, feature_count = image_rows.shape
    owned_rows = text_rows.shape[0]
    length = owned_rows * member_count
    window_tiles = max(1, owned_rows // TR)
    capacity = piece_rows * window_tiles
    row_groups = lax.dynamic_slice_in_dim(tile_group, my_group * tiles_row, tiles_row)
    chooser = (row_groups[None, :] == jnp.arange(group_count, dtype=jnp.int32)[:, None]).astype(
        jnp.bfloat16
    )
    outgoing = jnp.einsum(
        "gj,jrd->grd", chooser, image_rows, preferred_element_type=jnp.float32
    ).astype(jnp.bfloat16)
    arrived = lax.all_to_all(outgoing, "dp", split_axis=0, concat_axis=0, tiled=True)
    table_group = tile_group.reshape(group_count, tiles_row)
    table_offset = tile_offset.reshape(group_count, tiles_row)
    matches = table_group == my_group
    present = jnp.any(matches, axis=1)
    offset_from = jnp.sum(jnp.where(matches, table_offset, 0), axis=1)
    within = jnp.arange(piece_rows, dtype=jnp.int32)
    landing = offset_from[:, None] + my_member * piece_rows + within[None, :]
    slot_index = offset_from[:, None] // TR % window_tiles * piece_rows + within[None, :]
    target = jnp.where(present[:, None], landing // owned_rows * capacity + slot_index, -1).reshape(
        -1
    )
    spread = (
        jnp.arange(member_count * capacity, dtype=jnp.int32)[:, None] == target[None, :]
    ).astype(jnp.bfloat16)
    forward = jnp.dot(
        spread,
        arrived.reshape(group_count * piece_rows, feature_count),
        preferred_element_type=jnp.float32,
    ).astype(jnp.bfloat16)
    landed = lax.all_to_all(
        forward.reshape(member_count, capacity, feature_count),
        "seq",
        split_axis=0,
        concat_axis=0,
        tiled=True,
    )
    positions = my_member * owned_rows + jnp.arange(owned_rows, dtype=jnp.int32)
    inside = (
        (tile_group[None, :] == my_group)
        & (tile_offset[None, :] <= positions[:, None])
        & (positions[:, None] < tile_offset[None, :] + TR)
    )
    covered = jnp.any(inside, axis=1)
    tile_start = jnp.sum(jnp.where(inside, tile_offset[None, :], 0), axis=1)
    offset_in = positions - tile_start
    source = (
        offset_in // piece_rows * capacity
        + tile_start // TR % window_tiles * piece_rows
        + offset_in % piece_rows
    )
    source = jnp.where(covered, source, 0)
    image_part = jnp.take(landed.reshape(member_count * capacity, feature_count), source, axis=0)
    merged = jnp.where(covered[:, None], image_part, text_rows)
    normed = rms_norm(merged, norm_gain)
    row_block = lax.all_gather(normed, "seq", axis=0, tiled=True)
    projected = jnp.concatenate(
        [
            jnp.dot(row_block, q_weight, preferred_element_type=jnp.float32),
            jnp.dot(row_block, k_weight, preferred_element_type=jnp.float32),
            jnp.dot(row_block, v_weight, preferred_element_type=jnp.float32),
        ],
        axis=1,
    )
    query_cols = q_weight.shape[1]
    half_cols = k_weight.shape[1]
    head_dim = 2 * half_cols
    query_raw = projected[:, :query_cols] + q_bias
    own_half = projected[:, query_cols:] + jnp.concatenate([k_bias, v_bias])
    other_half = swapped(own_half, "seq", 0)
    is_lower = my_member % 2 == 0
    lower_half = jnp.where(is_lower, own_half, other_half)
    upper_half = jnp.where(is_lower, other_half, own_half)
    key_raw = jnp.concatenate([lower_half[:, :half_cols], upper_half[:, :half_cols]], axis=1)
    value_rows = jnp.concatenate(
        [lower_half[:, half_cols:], upper_half[:, half_cols:]], axis=1
    ).astype(jnp.bfloat16)
    doc_row = doc_ids[0]
    in_doc = doc_positions(doc_row)
    queries = rotary(query_raw.reshape(length, query_cols // head_dim, head_dim), in_doc).astype(
        jnp.bfloat16
    )
    key_rows = rotary(key_raw, in_doc).astype(jnp.bfloat16)
    return attend(queries, key_rows, value_rows, doc_row, seq_len[0])


def solution(mesh):
    return jax.shard_map(
        per_device,
        mesh=mesh,
        in_specs=(
            P(("dp", "seq"), None),
            P("dp", "seq", None),
            P(),
            P(),
            P("dp"),
            P("dp", None),
            P(),
            P(None, "seq"),
            P(None, "seq"),
            P(None, "seq"),
            P("seq"),
            P("seq"),
            P("seq"),
        ),
        out_specs=P("dp", "seq"),
        check_vma=False,
    )
```

profile of v0, /device:TPU:1, one launch (start us, length us, event | category | flops | bytes accessed | tf_op | source)
XLA Modules:
  0.0 477.6 jit_solution(18265404585857604997)
XLA Ops:
  7.8 1.5 convolution_convert_fusion.1
  9.3 2.5 copy.45
  11.7 5.8 %all-to-all-start = ((bf16[8,16,8192]{2,1,0:T(8,128)(2,1)}), bf16[8,16,8192]{2,1,0:T(8,128)(2,1)S(1)}, u32[]{:S(2)}, u32[]{:S(2)}) async-start(bf16[8,16,8192]{2,1,0:T(8,128)(2,1)} %copy.45), calls=%async_computation | async-start | bytes 4194304 | tf_op jit(solution)/shard_map/all_to_all | solution.py:124
  18.4 25.3 %all-to-all-done = bf16[8,16,8192]{2,1,0:T(8,128)(2,1)S(1)} async-done(((bf16[8,16,8192]{2,1,0:T(8,128)(2,1)}), bf16[8,16,8192]{2,1,0:T(8,128)(2,1)S(1)}, u32[]{:S(2)}, u32[]{:S(2)}) %all-to-all-start) | async-done | bytes 2097184 | tf_op jit(solution)/shard_map/all_to_all | solution.py:124
  43.7 3.2 convolution_convert_fusion
  47.0 7.8 %all-to-all-start.1 = ((bf16[16,16,8192]{2,1,0:T(8,128)(2,1)}), bf16[16,16,8192]{2,1,0:T(8,128)(2,1)}, u32[]{:S(2)}, u32[]{:S(2)}) async-start(bf16[16,16,8192]{2,1,0:T(8,128)(2,1)} %bitcast.73), calls=%async_computation.1 | async-start | bytes 8388608 | tf_op jit(solution)/shard_map/all_to_all | solution.py:144
  55.1 61.4 %all-to-all-done.1 = bf16[16,16,8192]{2,1,0:T(8,128)(2,1)} async-done(((bf16[16,16,8192]{2,1,0:T(8,128)(2,1)}), bf16[16,16,8192]{2,1,0:T(8,128)(2,1)}, u32[]{:S(2)}, u32[]{:S(2)}) %all-to-all-start.1) | async-done | bytes 4194336 | tf_op jit(solution)/shard_map/all_to_all | solution.py:144
  116.6 6.5 %gather_fusion = bf16[128,8192]{1,0:T(8,128)(2,1)S(1)} fusion(bf16[256,8192]{1,0:T(8,128)(2,1)} %bitcast.9, s32[1024]{0:T(1024)S(1)} %pad_clamp_fusion), kind=kCustom, calls=%fused_computation | custom fusion | bytes 4194816 | tf_op jit(solution)/shard_map/jit(_take)/gather | solution.py:166
  123.1 2.8 fusion.34
  125.9 1.9 fusion.36
  128.8 3.0 multiply_cosine_fusion
  131.7 192.0 %all-gather.2.cloned.1.call-done = bf16[2048,8192]{1,0:T(8,128)(2,1)} async-done(((bf16[128,8192]{1,0:T(8,128)(2,1)}), bf16[2048,8192]{1,0:T(8,128)(2,1)}) %all-gather.2.cloned.1.call-update) | async-done | bytes 33554448 | tf_op jit(solution)/shard_map/all_gather | solution.py:169
  323.7 16.2 %fusion.65 = f32[2048,64]{0,1:T(8,128)S(1)} fusion(bf16[2048,8192]{1,0:T(8,128)(2,1)} %all-gather.2.cloned.1.call-done, bf16[8192,64]{0,1:T(8,128)(2,1)S(1)} %copy-done.5), kind=kOutput, calls=%fused_computation.114 | convolution fusion | flops 2147483648 | bytes 35127296 | tf_op jit(solution)/shard_map/dot_general | solution.py:174
  339.9 16.2 %fusion.64 = f32[2048,64]{0,1:T(8,128)S(1)} fusion(bf16[2048,8192]{1,0:T(8,128)(2,1)} %all-gather.2.cloned.1.call-done, bf16[8192,64]{0,1:T(8,128)(2,1)S(1)} %copy-done.6), kind=kOutput, calls=%fused_computation.113 | convolution fusion | flops 2147483648 | bytes 35127296 | tf_op jit(solution)/shard_map/dot_general | solution.py:173
  356.2 1.3 collective-permute-start
  357.5 25.0 %convolution_add_fusion = f32[2048,512]{0,1:T(8,128)} fusion(bf16[2048,8192]{1,0:T(8,128)(2,1)} %all-gather.2.cloned.1.call-done, bf16[8192,512]{1,0:T(8,128)(2,1)} %param.22, f32[512]{0:T(512)S(1)} %copy-done.10), kind=kOutput, calls=%fused_computation.43 | convolution fusion | flops 17180917760 | bytes 46139392 | tf_op jit(solution)/shard_map/dot_general | solution.py:172
  382.5 5.3 %copy.47 = f32[2048,4,128]{2,0,1:T(8,128)} copy(f32[2048,4,128]{0,2,1:T(8,128)} %bitcast.76) | data formatting | bytes 8388608 | tf_op jit(solution)/shard_map/reshape | solution.py:193
  387.8 7.9 %slice_negate_fusion = (f32[2048,4,64]{2,0,1:T(8,128)}, f32[2048,4,64]{2,0,1:T(8,128)}) fusion(f32[2048,4,128]{2,0,1:T(8,128)} %copy.47), kind=kLoop, calls=%fused_computation.39 | loop fusion | flops 524288 | bytes 8388608 | tf_op jit(solution)/shard_map/neg | solution.py:45
  398.7 1.9 fusion.44
  400.6 2.0 concatenate.52
  402.5 7.1 %fusion.38 = bf16[2048,4,128]{2,0,1:T(8,128)(2,1)} fusion(f32[2048,4,64]{2,0,1:T(8,128)} %get-tuple-element.221, f32[2048,4,64]{2,0,1:T(8,128)} %get-tuple-element.220, f32[2048,4,128]{2,0,1:T(8,128)} %copy.47, f32[2048,128]{1,0:T(8,128)S(1)} %copy.50, f32[2048,128]{1,0:T(8,128)S(1)} %copy.46), kind=kLoop, calls=%fused_computation.42 | loop fusion | flops 5242880 | bytes 12582912 | tf_op jit(solution)/shard_map/convert_element_type | solution.py:193
  409.8 58.4 %while.13 = (s32[]{:T(128)}, bf16[2048,512]{1,0:T(8,128)(2,1)S(1)}, s32[]{:T(128)}, bf16[2560,128]{0,1:T(8,128)(2,1)}, s32[2048]{0:T(1024)S(1)}, /*index=5*/s32[...) while((s32[]{:T(128)}, bf16[2048,512]{1,0:T(8,128)(2,1)S(1)}, ...), condition=%wide.region_10.11_spmd, body=%wide.region_7.10_spmd.sunk | while | flops 1088949760 | bytes 21550328 | solution.py:90
  412.6 7.5 %fusion.81 = (f32[4,512]{1,0:T(4,128)S(1)}, f32[4,512,1024]{1,2,0:T(8,128)}) fusion(pred[512,1024]{0,1:T(8,128)(4,1)S(1)} %and_and_fusion.2, bf16[2048,4,128]{2,0,1:T(8,128)(2,1)} %get-tuple-element.330, s32[]{:T(128)S(6)} %select_n.269, bf16[2560,128]{0,1:T(8,128)(2,1)} %get-tuple-element.329, s32[]{:T(128)S(6)} %select_n.270), kind=kOutput, calls=%fused_computation.112.clone.1 | convolution fusion | flops 545260544 | bytes 9707528 | tf_op jit(solution)/shard_map/while/body/eval_jaxpr/sub | solution.py:81
  420.1 4.2 fusion.82
  427.1 7.6 %fusion.81 = (f32[4,512]{1,0:T(4,128)S(1)}, f32[4,512,1024]{1,2,0:T(8,128)}) fusion(pred[512,1024]{0,1:T(8,128)(4,1)S(1)} %and_and_fusion.2, bf16[2048,4,128]{2,0,1:T(8,128)(2,1)} %get-tuple-element.330, s32[]{:T(128)S(6)} %select_n.269, bf16[2560,128]{0,1:T(8,128)(2,1)} %get-tuple-element.329, s32[]{:T(128)S(6)} %select_n.270), kind=kOutput, calls=%fused_computation.112.clone.1 | convolution fusion | flops 545260544 | bytes 9707528 | tf_op jit(solution)/shard_map/while/body/eval_jaxpr/sub | solution.py:81
  434.6 4.2 fusion.82
  441.6 7.5 %fusion.81 = (f32[4,512]{1,0:T(4,128)S(1)}, f32[4,512,1024]{1,2,0:T(8,128)}) fusion(pred[512,1024]{0,1:T(8,128)(4,1)S(1)} %and_and_fusion.2, bf16[2048,4,128]{2,0,1:T(8,128)(2,1)} %get-tuple-element.330, s32[]{:T(128)S(6)} %select_n.269, bf16[2560,128]{0,1:T(8,128)(2,1)} %get-tuple-element.329, s32[]{:T(128)S(6)} %select_n.270), kind=kOutput, calls=%fused_computation.112.clone.1 | convolution fusion | flops 545260544 | bytes 9707528 | tf_op jit(solution)/shard_map/while/body/eval_jaxpr/sub | solution.py:81
  449.2 4.2 fusion.82
  456.2 7.5 %fusion.81 = (f32[4,512]{1,0:T(4,128)S(1)}, f32[4,512,1024]{1,2,0:T(8,128)}) fusion(pred[512,1024]{0,1:T(8,128)(4,1)S(1)} %and_and_fusion.2, bf16[2048,4,128]{2,0,1:T(8,128)(2,1)} %get-tuple-element.330, s32[]{:T(128)S(6)} %select_n.269, bf16[2560,128]{0,1:T(8,128)(2,1)} %get-tuple-element.329, s32[]{:T(128)S(6)} %select_n.270), kind=kOutput, calls=%fused_computation.112.clone.1 | convolution fusion | flops 545260544 | bytes 9707528 | tf_op jit(solution)/shard_map/while/body/eval_jaxpr/sub | solution.py:81
  463.7 4.2 fusion.82
  468.2 1.3 copy-done.2
  469.5 1.2 copy-done.1
  (104 shorter events, 17.3 us)
Async XLA Ops:
  6.5 1.2 copy-start
  9.2 8.3 %copy-start.11 = (s32[32]{0:T(128)S(1)}, s32[32]{0:T(128)}, u32[]{:S(2)}) copy-start(s32[32]{0:T(128)} %param.17) | copy-start | bytes 388
  9.3 8.7 %copy-start.9 = (s32[32]{0:T(128)S(1)}, s32[32]{0:T(128)}, u32[]{:S(2)}) copy-start(s32[32]{0:T(128)} %param.18) | copy-start | bytes 388
  11.7 32.0 %all-to-all-start = ((bf16[8,16,8192]{2,1,0:T(8,128)(2,1)}), bf16[8,16,8192]{2,1,0:T(8,128)(2,1)S(1)}, u32[]{:S(2)}, u32[]{:S(2)}) async-start(bf16[8,16,8192]{2,1,0:T(8,128)(2,1)} %copy.45), calls=%async_computation | async-start | bytes 4194304 | tf_op jit(solution)/shard_map/all_to_all | solution.py:124
  47.0 69.6 %all-to-all-start.1 = ((bf16[16,16,8192]{2,1,0:T(8,128)(2,1)}), bf16[16,16,8192]{2,1,0:T(8,128)(2,1)}, u32[]{:S(2)}, u32[]{:S(2)}) async-start(bf16[16,16,8192]{2,1,0:T(8,128)(2,1)} %bitcast.73), calls=%async_computation.1 | async-start | bytes 8388608 | tf_op jit(solution)/shard_map/all_to_all | solution.py:144
  54.8 268.9 %all-gather.2.cloned.1.call-start = ((), (), s32[]{:S(2)}) async-start(), calls=%async_computation.2 | async-start | bytes 35651584 | tf_op jit(solution)/shard_map/all_gather | solution.py:169
  123.0 2.9 copy-start.8
  125.9 2.0 copy-start.7
  125.9 2.6 copy-start.12
  125.9 2.6 copy-start.13
  125.9 197.8 %copy-start.5 = (bf16[8192,64]{0,1:T(8,128)(2,1)S(1)}, bf16[8192,64]{0,1:T(8,128)(2,1)}, u32[]{:S(2)}) copy-start(bf16[8192,64]{0,1:T(8,128)(2,1)} %param.24) | copy-start | bytes 3145732
  131.7 208.1 %copy-start.6 = (bf16[8192,64]{0,1:T(8,128)(2,1)S(1)}, bf16[8192,64]{0,1:T(8,128)(2,1)}, u32[]{:S(2)}) copy-start(bf16[8192,64]{0,1:T(8,128)(2,1)} %param.23) | copy-start | bytes 3145732
  339.9 17.6 %copy-start.10 = (f32[512]{0:T(512)S(1)}, f32[512]{0:T(512)}, u32[]{:S(2)}) copy-start(f32[512]{0:T(512)} %param.25) | copy-start | bytes 6148
  356.2 39.5 %collective-permute-start = (f32[2048,128]{0,1:T(8,128)S(1)}, f32[2048,128]{0,1:T(8,128)S(1)}, u32[]{:S(2)}, u32[]{:S(2)}) collective-permute-start(f32[2048,128]{0,1:T(8,128)S(1)} %maximum_add_fusion), channel_id=1, source_target_pairs={{0,1},{1,0},{2,3},{3,2},{4,5},{5,4},{6,7},{7,6},{8,9},{9,8},{10,11... | collective-permute-start | bytes 3145736 | tf_op jit(solution)/shard_map/ppermute | solution.py:19
  395.8 1.1 copy-start.3
  395.8 1.2 copy-start.4
  468.2 1.3 copy-start.2
  469.5 1.2 copy-start.1
Sparse Core Ops, SparseCore 0:
  128.0 195.6 all-gather.1
where the time goes:
time: 478 us
  waiting for transfers between devices  279 us (58%)
  matrix products  109 us (23%)
  other arithmetic  36.5 us (8%)
  local copies, waits for them, and re-layouts  24.2 us (5%)
  starting transfers between devices  14.9 us (3%)
  between operations  13.7 us (3%)
    all_gather x1, waiting for transfers between devices, per_device(): row_block = lax.all_gather(normed, 'seq', axis=0, tiled=True)  192 us
    all_to_all x1, waiting for transfers between devices, per_device(): lax.all_to_all(forward.reshape(member_count, capacity, feature_count), 's...  61.4 us
    sub x4, matrix products, one_block(): exponent = jnp.exp(scores - row_peak)  30.2 us
    all_to_all x1, waiting for transfers between devices, per_device(): lax.all_to_all(outgoing, 'dp', split_axis=0, concat_axis=0, tiled=True)  25.3 us
    dot_general x1, matrix products, per_device(): jnp.dot(row_block, q_weight, preferred_element_type=jnp.float32)  25 us
    dot_general x4, matrix products, one_block(): jnp.einsum('hqk,kd->qhd', weights, value_part, preferred_element_type=jnp...  16.9 us
    dot_general x1, matrix products, per_device(): jnp.dot(row_block, k_weight, preferred_element_type=jnp.float32)  16.2 us
    dot_general x1, matrix products, per_device(): jnp.dot(row_block, v_weight, preferred_element_type=jnp.float32)  16.2 us
  transfers between devices with their start and end apart: 4, of which 3 were waited for; matrix products, arithmetic and copies ran while one was open for 9% of the time, Pallas kernels for 0%

commit v1 on v0

--- a/solution.py
+++ b/solution.py
@@ -166,7 +166,9 @@
     image_part = jnp.take(landed.reshape(member_count * capacity, feature_count), source, axis=0)
     merged = jnp.where(covered[:, None], image_part, text_rows)
     normed = rms_norm(merged, norm_gain)
-    row_block = lax.all_gather(normed, "seq", axis=0, tiled=True)
+    row_block = jnp.concatenate(
+        lax.all_to_all(jnp.stack([normed] * lax.axis_size("seq")), "seq", 0, 0), axis=0
+    )
     projected = jnp.concatenate(
         [
             jnp.dot(row_block, q_weight, preferred_element_type=jnp.float32),

time: 478 us -> 781 us (1.63)
  waiting for transfers between devices: 279 us -> 578 us
  between operations: 13.7 us -> 0.35 us
  local copies, waits for them, and re-layouts: 24.2 us -> 35.1 us
    all_to_all x0 -> x1, waiting for transfers between devices: none -> 491 us  [per_device(): lax.all_to_all(jnp.stack([normed] * lax.axis_size('seq')), 'seq', 0, 0)]
    all_gather x1 -> x0, waiting for transfers between devices: 192 us -> none  [per_device(): row_block = lax.all_gather(normed, 'seq', axis=0, tiled=True)]
    another operation x1 -> x2, local copies, waits for them, and re-layouts: 0.11 us -> 11.1 us  [the longest x1 11 us: per_device(): jnp.stack([normed] * lax.axis_size('seq'))]
  transfers between devices with their start and end apart: 4 -> 4, of which waited for: 3 -> 3; matrix products, arithmetic and copies ran while one was open for 9% -> 6% of each run, Pallas kernels for 0% -> 0%
where the time goes in v1:
time: 781 us; the launch traced here: 778 us
  waiting for transfers between devices  578 us (74%)
  matrix products  109 us (14%)
  local copies, waits for them, and re-layouts  35.1 us (4%)
  other arithmetic  34.9 us (4%)
  starting transfers between devices  20.2 us (3%)
    all_to_all x1, waiting for transfers between devices, per_device(): lax.all_to_all(jnp.stack([normed] * lax.axis_size('seq')), 'seq', 0, 0)  491 us
    all_to_all x1, waiting for transfers between devices, per_device(): lax.all_to_all(forward.reshape(member_count, capacity, feature_count), 's...  61.5 us
    sub x4, matrix products, one_block(): exponent = jnp.exp(scores - row_peak)  30.2 us
    all_to_all x1, waiting for transfers between devices, per_device(): lax.all_to_all(outgoing, 'dp', split_axis=0, concat_axis=0, tiled=True)  25.3 us
    dot_general x1, matrix products, per_device(): jnp.dot(row_block, q_weight, preferred_element_type=jnp.float32)  25 us
    dot_general x4, matrix products, one_block(): jnp.einsum('hqk,kd->qhd', weights, value_part, preferred_element_type=jnp...  16.9 us
    dot_general x1, matrix products, per_device(): jnp.dot(row_block, k_weight, preferred_element_type=jnp.float32)  16.3 us
    dot_general x1, matrix products, per_device(): jnp.dot(row_block, v_weight, preferred_element_type=jnp.float32)  16.2 us
  transfers between devices with their start and end apart: 4, of which 3 were waited for; matrix products, arithmetic and copies ran while one was open for 6% of the time, Pallas kernels for 0%

profile of v1, /device:TPU:1, one launch (start us, length us, event | category | flops | bytes accessed | tf_op | source)
XLA Modules:
  0.0 778.4 jit_solution(7467490565654643099)
XLA Ops:
  1.2 1.5 convolution_convert_fusion.1
  2.7 2.5 copy.45
  5.2 5.8 all-to-all-start
  11.9 25.3 %all-to-all-done = bf16[8,16,8192]{2,1,0:T(8,128)(2,1)S(1)} async-done(((bf16[8,16,8192]{2,1,0:T(8,128)(2,1)}), bf16[8,16,8192]{2,1,0:T(8,128)(2,1)S(1)}, u32[]{:S(2)}, u32[]{:S(2)}) %all-to-all-start) | async-done | bytes 2097184 | tf_op jit(solution)/shard_map/all_to_all | solution.py:124
  37.2 3.2 convolution_convert_fusion
  40.4 7.8 %all-to-all-start.1 = ((bf16[16,16,8192]{2,1,0:T(8,128)(2,1)}), bf16[16,16,8192]{2,1,0:T(8,128)(2,1)}, u32[]{:S(2)}, u32[]{:S(2)}) async-start(bf16[16,16,8192]{2,1,0:T(8,128)(2,1)} %bitcast.74), calls=%async_computation.1 | async-start | bytes 8388608 | tf_op jit(solution)/shard_map/all_to_all | solution.py:144
  48.5 61.5 %all-to-all-done.1 = bf16[16,16,8192]{2,1,0:T(8,128)(2,1)} async-done(((bf16[16,16,8192]{2,1,0:T(8,128)(2,1)}), bf16[16,16,8192]{2,1,0:T(8,128)(2,1)}, u32[]{:S(2)}, u32[]{:S(2)}) %all-to-all-start.1) | async-done | bytes 4194336 | tf_op jit(solution)/shard_map/all_to_all | solution.py:144
  110.0 6.5 gather_fusion
  116.5 2.8 fusion.34
  119.9 11.0 %stack.2 = bf16[16,128,8192]{2,1,0:T(8,128)(2,1)} broadcast(bf16[128,8192]{1,0:T(8,128)(2,1)S(1)} %fusion.36), dimensions={1,2} | broadcast | bytes 35651584 | tf_op jit(solution)/shard_map/stack | solution.py:170
  130.9 6.3 all-to-all-start.2
  138.1 2.8 multiply_cosine_fusion
  140.9 491.3 %all-to-all-done.2 = bf16[16,128,8192]{2,1,0:T(8,128)(2,1)} async-done(((bf16[16,128,8192]{2,1,0:T(8,128)(2,1)}), bf16[16,128,8192]{2,1,0:T(8,128)(2,1)}, u32[]{:S(2)}, u32[]{:S(2)}) %all-to-all-start.2) | async-done | bytes 33554464 | tf_op jit(solution)/shard_map/all_to_all | solution.py:170
  632.2 16.3 %fusion.64 = f32[2048,64]{0,1:T(8,128)S(1)} fusion(bf16[2048,8192]{1,0:T(8,128)(2,1)} %bitcast.13, bf16[8192,64]{0,1:T(8,128)(2,1)S(1)} %copy-done.5), kind=kOutput, calls=%fused_computation.113 | convolution fusion | flops 2147483648 | bytes 35127296 | tf_op jit(solution)/shard_map/dot_general | solution.py:175
  648.5 16.2 %fusion.65 = f32[2048,64]{0,1:T(8,128)S(1)} fusion(bf16[2048,8192]{1,0:T(8,128)(2,1)} %bitcast.13, bf16[8192,64]{0,1:T(8,128)(2,1)S(1)} %copy-done.6), kind=kOutput, calls=%fused_computation.114 | convolution fusion | flops 2147483648 | bytes 35127296 | tf_op jit(solution)/shard_map/dot_general | solution.py:176
  665.1 25.0 %convolution_add_fusion = f32[2048,512]{0,1:T(8,128)} fusion(bf16[2048,8192]{1,0:T(8,128)(2,1)} %bitcast.13, bf16[8192,512]{1,0:T(8,128)(2,1)} %param.22, f32[512]{0:T(512)S(1)} %copy-done.10), kind=kOutput, calls=%fused_computation.43 | convolution fusion | flops 17180917760 | bytes 46139392 | tf_op jit(solution)/shard_map/dot_general | solution.py:174
  690.1 5.3 copy.47
  695.4 7.9 %slice_negate_fusion = (f32[2048,4,64]{2,0,1:T(8,128)}, f32[2048,4,64]{2,0,1:T(8,128)}) fusion(f32[2048,4,128]{2,0,1:T(8,128)} %copy.47), kind=kLoop, calls=%fused_computation.39 | loop fusion | flops 524288 | bytes 8388608 | tf_op jit(solution)/shard_map/neg | solution.py:45
  706.3 2.0 concatenate.52
  708.3 1.9 fusion.44
  710.2 7.1 fusion.38
  717.4 58.4 %while.13 = (s32[]{:T(128)}, bf16[2048,512]{1,0:T(8,128)(2,1)S(1)}, s32[]{:T(128)}, bf16[2560,128]{0,1:T(8,128)(2,1)}, s32[2048]{0:T(1024)S(1)}, /*index=5*/s32[...) while((s32[]{:T(128)}, bf16[2048,512]{1,0:T(8,128)(2,1)S(1)}, ...), condition=%wide.region_10.11_spmd, body=%wide.region_7.10_spmd.sunk | while | flops 1088949760 | bytes 21550328 | solution.py:90
  719.5 7.6 fusion.81
  727.7 4.2 fusion.82
  734.1 7.5 fusion.81
  742.2 4.2 fusion.82
  748.6 7.6 fusion.81
  756.8 4.2 fusion.82
  763.1 7.5 fusion.81
  771.3 4.2 fusion.82
  775.8 1.3 copy-done.2
  777.1 1.2 copy-done.1
  (104 shorter events, 18.1 us)
Async XLA Ops:
  0.0 1.2 copy-start
  2.7 8.3 %copy-start.11 = (s32[32]{0:T(128)S(1)}, s32[32]{0:T(128)}, u32[]{:S(2)}) copy-start(s32[32]{0:T(128)} %param.17) | copy-start | bytes 388
  2.7 8.4 %copy-start.9 = (s32[32]{0:T(128)S(1)}, s32[32]{0:T(128)}, u32[]{:S(2)}) copy-start(s32[32]{0:T(128)} %param.18) | copy-start | bytes 388
  5.2 32.0 %all-to-all-start = ((bf16[8,16,8192]{2,1,0:T(8,128)(2,1)}), bf16[8,16,8192]{2,1,0:T(8,128)(2,1)S(1)}, u32[]{:S(2)}, u32[]{:S(2)}) async-start(bf16[8,16,8192]{2,1,0:T(8,128)(2,1)} %copy.45), calls=%async_computation | async-start | bytes 4194304 | tf_op jit(solution)/shard_map/all_to_all | solution.py:124
  40.4 69.6 %all-to-all-start.1 = ((bf16[16,16,8192]{2,1,0:T(8,128)(2,1)}), bf16[16,16,8192]{2,1,0:T(8,128)(2,1)}, u32[]{:S(2)}, u32[]{:S(2)}) async-start(bf16[16,16,8192]{2,1,0:T(8,128)(2,1)} %bitcast.74), calls=%async_computation.1 | async-start | bytes 8388608 | tf_op jit(solution)/shard_map/all_to_all | solution.py:144
  116.5 2.8 copy-start.8
  130.9 6.3 copy-start.7
  130.9 6.9 copy-start.12
  130.9 6.9 copy-start.13
  130.9 501.3 %copy-start.5 = (bf16[8192,64]{0,1:T(8,128)(2,1)S(1)}, bf16[8192,64]{0,1:T(8,128)(2,1)}, u32[]{:S(2)}) copy-start(bf16[8192,64]{0,1:T(8,128)(2,1)} %param.23) | copy-start | bytes 3145732
  130.9 501.3 %all-to-all-start.2 = ((bf16[16,128,8192]{2,1,0:T(8,128)(2,1)}), bf16[16,128,8192]{2,1,0:T(8,128)(2,1)}, u32[]{:S(2)}, u32[]{:S(2)}) async-start(bf16[16,128,8192]{2,1,0:T(8,128)(2,1)} %stack.2), calls=%async_computation.2 | async-start | bytes 67108864 | tf_op jit(solution)/shard_map/all_to_all | solution.py:170
  632.2 16.3 %copy-start.6 = (bf16[8192,64]{0,1:T(8,128)(2,1)S(1)}, bf16[8192,64]{0,1:T(8,128)(2,1)}, u32[]{:S(2)}) copy-start(bf16[8192,64]{0,1:T(8,128)(2,1)} %param.24) | copy-start | bytes 3145732
  648.5 16.7 %copy-start.10 = (f32[512]{0:T(512)S(1)}, f32[512]{0:T(512)}, u32[]{:S(2)}) copy-start(f32[512]{0:T(512)} %param.25) | copy-start | bytes 6148
  664.8 38.6 %collective-permute-start = (f32[2048,128]{0,1:T(8,128)S(1)}, f32[2048,128]{0,1:T(8,128)S(1)}, u32[]{:S(2)}, u32[]{:S(2)}) collective-permute-start(f32[2048,128]{0,1:T(8,128)S(1)} %maximum_add_fusion), channel_id=1, source_target_pairs={{0,1},{1,0},{2,3},{3,2},{4,5},{5,4},{6,7},{7,6},{8,9},{9,8},{10,11... | collective-permute-start | bytes 3145736 | tf_op jit(solution)/shard_map/ppermute | solution.py:19
  703.4 1.1 copy-start.3
  703.4 1.2 copy-start.4
  775.8 1.3 copy-start.2
  777.1 1.2 copy-start.1
